TPU v7x, 32 devices: a whole 2x2x4 slice. The times are simulated.
32 devices in a mesh: grp: 4 (over z), sp: 8 (over y, x, core).
Axes of the slice: x: 2, y: 2, z: 4, core: 2. Of those that a mesh axis runs over, the one named last changes fastest.
Arguments:
- tokens: bfloat16 [2048, 2880], P(('grp', 'sp')), may hold values from -36 to 36
- query_weight: bfloat16 [2880, 2048], P(None, 'sp'), may hold values from -0.109375 to 0.109375
- key_value_weight: bfloat16 [2880, 1024], replicated, may hold values from -0.109375 to 0.109375
- block_places: int32 [16], replicated, may hold values from 0 to 15, each once
- sinks: float32 [32], replicated, may hold values from -1 to 5
Outputs:
- attended: bfloat16 [2048, 2048], P(('grp', 'sp'))
Inputs may be any that keep to these rules, and one draw needn't show every extreme that they name: `block_places`: every sequence block appears once.
All inputs are finite; a program needn't handle non-finite values.
Results may differ from a plain program's by a relative error of at most 0.008.
The roundings to bfloat16 on the way count: a program that leaves them out, or rounds other values in their place, can miss the bound.
Values may be sent and summed in bfloat16 or wider, within the bound.
A program may use at most 128 MiB of HBM per device.

v0:
```python
import jax
import jax.numpy as jnp
from jax import lax
from jax.sharding import PartitionSpec as P

QUERY_HEADS = 32
HEAD_SIZE = 64
BPG = 4
rope_base = 150000.0
neg_large = -1e30


def rotate(vectors, angles):
    middle = vectors.shape[-1] // 2
    first_half = vectors[..., :middle]
    second_half = vectors[..., middle:]
    cosine = jnp.cos(angles)
    sine_part = jnp.sin(angles)
    return jnp.concatenate(
        [
            first_half * cosine - second_half * sine_part,
            second_half * cosine + first_half * sine_part,
        ],
        axis=-1,
    )


def locate(stored, block_rows, block_places):
    blocks = stored // block_rows
    table = jnp.arange(block_places.shape[0], dtype=jnp.int32)
    onehot = (blocks[:, None] == table[None, :]).astype(jnp.int32)
    return jnp.sum(onehot * block_places[None, :], axis=1) * block_rows + stored % block_rows


def prepare(projected, own_places, query_cols, kv_cols, head_count):
    row_count = projected.shape[0]
    inverse = rope_base ** (-(jnp.arange(HEAD_SIZE // 2, dtype=jnp.float32) * 2.0) / HEAD_SIZE)
    angles = own_places.astype(jnp.float32)[:, None, None] * inverse[None, None, :]
    queries = rotate(
        projected[:, :query_cols].reshape(row_count, query_cols // HEAD_SIZE, HEAD_SIZE), angles
    ).astype(jnp.bfloat16)
    rotated_keys = rotate(
        projected[:, query_cols : query_cols + kv_cols].reshape(row_count, head_count, HEAD_SIZE),
        angles,
    )
    key_value_pair = jnp.concatenate(
        [rotated_keys.reshape(row_count, kv_cols), projected[:, query_cols + kv_cols :]], axis=1
    ).astype(jnp.bfloat16)
    return (queries, key_value_pair)


def attend(state, queries, query_places, key_value_pair, key_places, head_count):
    maxima, totals, mixture = state
    key_count = key_value_pair.shape[0]
    column_half = key_value_pair.shape[1] // 2
    key_part = key_value_pair[:, :column_half].reshape(key_count, head_count, HEAD_SIZE)
    value_part = key_value_pair[:, column_half:].reshape(key_count, head_count, HEAD_SIZE)
    scores = jnp.einsum(
        "qhgd,khd->hgqk", queries, key_part, preferred_element_type=jnp.float32
    ) * HEAD_SIZE ** (-0.5)
    allowed = key_places[None, :] <= query_places[:, None]
    scores = jnp.where(allowed, scores, neg_large)
    updated = jnp.maximum(maxima, jnp.max(scores, axis=-1))
    weights = jnp.where(allowed, jnp.exp(scores - updated[..., None]), 0.0)
    factor = jnp.exp(maxima - updated)
    totals = totals * factor + jnp.sum(weights, axis=-1)
    mixture = mixture * factor[..., None] + jnp.einsum(
        "hgqk,khd->hgqd",
        weights.astype(jnp.bfloat16),
        value_part,
        preferred_element_type=jnp.float32,
    )
    return (updated, totals, mixture)


def per_device(tokens, query_weight, key_value_weight, block_places, sinks):
    sp_count = lax.axis_size("sp")
    local_rows = tokens.shape[0]
    group_rows = local_rows * sp_count
    block_rows = group_rows // BPG
    kv_total = key_value_weight.shape[1] // (2 * HEAD_SIZE)
    sp_place = lax.axis_index("sp")
    grp_place = lax.axis_index("grp")
    query_cols = query_weight.shape[1]
    query_heads = query_cols // HEAD_SIZE
    head_count = max(kv_total // sp_count, 1)
    kv_cols = head_count * HEAD_SIZE
    first_head = sp_place * query_heads // (QUERY_HEADS // kv_total)
    key_weight = lax.dynamic_slice_in_dim(key_value_weight, first_head * HEAD_SIZE, kv_cols, 1)
    value_weight = lax.dynamic_slice_in_dim(
        key_value_weight, kv_total * HEAD_SIZE + first_head * HEAD_SIZE, kv_cols, 1
    )
    joined = jnp.concatenate([query_weight, key_weight, value_weight], axis=1)
    projected = jnp.dot(
        lax.all_gather(tokens, "sp", axis=0, tiled=True), joined, preferred_element_type=jnp.float32
    )
    query_local = jnp.arange(group_rows, dtype=jnp.int32)
    head_first = sp_place * query_heads
    own_places = locate(grp_place * group_rows + query_local, block_rows, block_places)
    queries, key_value_pair = prepare(projected, own_places, query_cols, kv_cols, head_count)
    query_sharing = query_heads // head_count
    head_sinks = lax.dynamic_slice_in_dim(sinks, head_first, query_heads, 0).reshape(
        head_count, query_sharing
    )
    sink_rows = jnp.broadcast_to(head_sinks[:, :, None], (head_count, query_sharing, group_rows))
    query_block4 = queries.reshape(group_rows, head_count, query_sharing, HEAD_SIZE)
    initial = (
        sink_rows,
        jnp.ones((head_count, query_sharing, group_rows), jnp.float32),
        jnp.zeros((head_count, query_sharing, group_rows, HEAD_SIZE), jnp.float32),
    )
    piece = lax.all_gather(key_value_pair, "grp", axis=0, tiled=True)
    step_rows = min(piece.shape[0], group_rows)
    turns = piece.shape[0] // step_rows

    def visit(turn, inner):
        offset = turn * step_rows
        piece_rows = lax.dynamic_slice_in_dim(piece, offset, step_rows, 0)
        position = offset + jnp.arange(step_rows, dtype=jnp.int32)
        stored = position // group_rows * group_rows + position % group_rows
        key_places = locate(stored, block_rows, block_places)
        return attend(inner, query_block4, own_places, piece_rows, key_places, head_count)

    maxima, totals, mixture = lax.fori_loop(0, turns, visit, initial)
    normed = jnp.transpose(mixture, (2, 0, 1, 3)) / jnp.transpose(totals, (2, 0, 1))[..., None]
    attended = normed.reshape(group_rows, query_cols).astype(jnp.bfloat16)
    return lax.all_to_all(attended, "sp", split_axis=0, concat_axis=1, tiled=True)


def solution(mesh):
    in_specs = (P(("grp", "sp"), None), P(None, "sp"), P(), P(), P())
    out_specs = P(("grp", "sp"), None)
    return jax.shard_map(
        per_device, mesh=mesh, in_specs=in_specs, out_specs=out_specs, check_vma=False
    )
```

profile of v0, /device:TPU:0, one launch (start us, length us, event | category | flops | bytes accessed | tf_op | source)
XLA Modules:
  0.0 114.0 jit_solution(16821734951300925589)
XLA Ops:
  6.5 0.7 all-gather.2.cloned.1.call-update
  7.3 0.7 dynamic_slice.20
  8.1 0.7 select_reduce_fusion.1
  8.8 0.3 multiply_cosine_fusion
  9.1 1.8 %constant_dynamic-slice_fusion.1 = (bf16[2880,64]{1,0:T(8,128)(2,1)S(1)}, bf16[2880,64]{1,0:T(8,128)(2,1)S(1)}) fusion(bf16[2880,1024]{1,0:T(8,128)(2,1)} %param.9, s32[]{:T(128)S(6)} %select_n.163, s32[]{:T(128)S(6)} %select_n.164), kind=kLoop, calls=%fused_computation.92 | loop fusion | bytes 1474568 | tf_op jit(solution)/shard_map/dynamic_slice | solution.py:89
  11.0 32.6 %all-gather.2.cloned.1.call-done = bf16[512,2880]{1,0:T(8,128)(2,1)} async-done(((bf16[64,2880]{1,0:T(8,128)(2,1)}), bf16[512,2880]{1,0:T(8,128)(2,1)}) %all-gather.2.cloned.1.call-update) | async-done | bytes 2949136 | tf_op jit(solution)/shard_map/all_gather | solution.py:95
  43.6 4.1 %fusion.32 = f32[512,384]{0,1:T(8,128)S(1)} fusion(bf16[512,2880]{1,0:T(8,128)(2,1)} %all-gather.2.cloned.1.call-done, bf16[2880,64]{1,0:T(8,128)(2,1)S(1)} %get-tuple-element.296, bf16[2880,64]{1,0:T(8,128)(2,1)S(1)} %get-tuple-element.295, bf16[2880,256]{1,0:T(8,128)(2,1)} %param.8), kind=kOutput, calls=%fused_computation.53 | convolution fusion | flops 1139097600 | bytes 5947392 | tf_op jit(solution)/shard_map/dot_general | solution.py:94
  47.8 0.3 fusion.43
  48.2 16.0 %all_gather.7 = bf16[2048,128]{0,1:T(8,128)(2,1)S(1)} all-gather(bf16[512,128]{0,1:T(8,128)(2,1)S(1)} %pad_maximum_fusion.1), channel_id=1, replica_groups=mesh['grp'=4,'sp'=8] {'grp'}, dimensions={0}, use_global_device_ids=true | all-gather | bytes 655360 | tf_op jit(solution)/shard_map/all_gather | solution.py:112
  64.4 31.9 %while.21 = (s32[]{:T(128)}, f32[1,4,512]{2,1,0:T(4,128)S(1)}, f32[1,4,512]{2,1,0:T(4,128)S(1)}, f32[1,4,512,64]{2,3,1,0:T(8,128)S(1)}, s32[16]{0:T(128)S(1)}, /...) while((s32[]{:T(128)}, f32[1,4,512]{2,1,0:T(4,128)S(1)}, ...), condition=%wide.region_5.6_spmd.clone, body=%wide.region_1.5_spmd.clone.sunk | while | flops 282791424 | bytes 31996208 | solution.py:124
  64.4 0.1 select_reduce_fusion.3
  64.5 0.2 broadcast_compare_fusion.3
  64.7 2.8 %fusion.62 = (f32[4,512]{1,0:T(4,128)S(1)}, f32[512,512,4]{1,0,2:T(8,128)}) fusion(pred[512,512]{0,1:T(8,128)(4,1)S(1)} %broadcast_compare_fusion.3, bf16[512,1,4,64]{0,3,2,1:T(8,128)(2,1)S(1)} %get-tuple-element.393, bf16[2048,128]{0,1:T(8,128)(2,1)S(1)} %get-tuple-element.392, s32[]{:T(128)S(6)} %select_n.256), kind=kOutput, calls=%fused_computation.2.clone.1 | convolution fusion | flops 137361408 | bytes 4792324 | tf_op jit(solution)/shard_map/while/body/eval_jaxpr/qhgd,khd->hgqk/dot_general | solution.py:58
  67.6 3.7 %fusion.65 = f32[1,4,512,64]{2,3,1,0:T(8,128)S(1)} fusion(f32[512,512,4]{1,0,2:T(8,128)} %get-tuple-element.358, f32[4,512]{1,0:T(4,128)S(1)} %bitcast.99, pred[512,512]{0,1:T(8,128)(4,1)S(1)} %broadcast_compare_fusion.3, f32[1,4,512,64]{2,3,1,0:T(8,128)S(1)} %get-tuple-element.376, f32[4,512]{1,0:T(4,128)S(1)} %get-tuple-element.359, ...), kind=kOutput, calls=%fused_computation.9.clone.1 | convolution fusion | flops 139853824 | bytes 5586953 | tf_op jit(solution)/shard_map/while/body/eval_jaxpr/hgqk,khd->hgqd/dot_general | solution.py:67
  71.3 1.0 fusion.64
  72.5 0.2 broadcast_compare_fusion.3
  72.7 2.8 %fusion.62 = (f32[4,512]{1,0:T(4,128)S(1)}, f32[512,512,4]{1,0,2:T(8,128)}) fusion(pred[512,512]{0,1:T(8,128)(4,1)S(1)} %broadcast_compare_fusion.3, bf16[512,1,4,64]{0,3,2,1:T(8,128)(2,1)S(1)} %get-tuple-element.393, bf16[2048,128]{0,1:T(8,128)(2,1)S(1)} %get-tuple-element.392, s32[]{:T(128)S(6)} %select_n.256), kind=kOutput, calls=%fused_computation.2.clone.1 | convolution fusion | flops 137361408 | bytes 4792324 | tf_op jit(solution)/shard_map/while/body/eval_jaxpr/qhgd,khd->hgqk/dot_general | solution.py:58
  75.6 3.7 %fusion.65 = f32[1,4,512,64]{2,3,1,0:T(8,128)S(1)} fusion(f32[512,512,4]{1,0,2:T(8,128)} %get-tuple-element.358, f32[4,512]{1,0:T(4,128)S(1)} %bitcast.99, pred[512,512]{0,1:T(8,128)(4,1)S(1)} %broadcast_compare_fusion.3, f32[1,4,512,64]{2,3,1,0:T(8,128)S(1)} %get-tuple-element.376, f32[4,512]{1,0:T(4,128)S(1)} %get-tuple-element.359, ...), kind=kOutput, calls=%fused_computation.9.clone.1 | convolution fusion | flops 139853824 | bytes 5586953 | tf_op jit(solution)/shard_map/while/body/eval_jaxpr/hgqk,khd->hgqd/dot_general | solution.py:67
  79.3 1.0 fusion.64
  80.4 0.1 select_reduce_fusion.3
  80.5 0.2 broadcast_compare_fusion.3
  80.7 2.8 %fusion.62 = (f32[4,512]{1,0:T(4,128)S(1)}, f32[512,512,4]{1,0,2:T(8,128)}) fusion(pred[512,512]{0,1:T(8,128)(4,1)S(1)} %broadcast_compare_fusion.3, bf16[512,1,4,64]{0,3,2,1:T(8,128)(2,1)S(1)} %get-tuple-element.393, bf16[2048,128]{0,1:T(8,128)(2,1)S(1)} %get-tuple-element.392, s32[]{:T(128)S(6)} %select_n.256), kind=kOutput, calls=%fused_computation.2.clone.1 | convolution fusion | flops 137361408 | bytes 4792324 | tf_op jit(solution)/shard_map/while/body/eval_jaxpr/qhgd,khd->hgqk/dot_general | solution.py:58
  83.5 3.7 %fusion.65 = f32[1,4,512,64]{2,3,1,0:T(8,128)S(1)} fusion(f32[512,512,4]{1,0,2:T(8,128)} %get-tuple-element.358, f32[4,512]{1,0:T(4,128)S(1)} %bitcast.99, pred[512,512]{0,1:T(8,128)(4,1)S(1)} %broadcast_compare_fusion.3, f32[1,4,512,64]{2,3,1,0:T(8,128)S(1)} %get-tuple-element.376, f32[4,512]{1,0:T(4,128)S(1)} %get-tuple-element.359, ...), kind=kOutput, calls=%fused_computation.9.clone.1 | convolution fusion | flops 139853824 | bytes 5586953 | tf_op jit(solution)/shard_map/while/body/eval_jaxpr/hgqk,khd->hgqd/dot_general | solution.py:67
  87.3 1.0 fusion.64
  88.5 0.2 broadcast_compare_fusion.3
  88.7 2.8 %fusion.62 = (f32[4,512]{1,0:T(4,128)S(1)}, f32[512,512,4]{1,0,2:T(8,128)}) fusion(pred[512,512]{0,1:T(8,128)(4,1)S(1)} %broadcast_compare_fusion.3, bf16[512,1,4,64]{0,3,2,1:T(8,128)(2,1)S(1)} %get-tuple-element.393, bf16[2048,128]{0,1:T(8,128)(2,1)S(1)} %get-tuple-element.392, s32[]{:T(128)S(6)} %select_n.256), kind=kOutput, calls=%fused_computation.2.clone.1 | convolution fusion | flops 137361408 | bytes 4792324 | tf_op jit(solution)/shard_map/while/body/eval_jaxpr/qhgd,khd->hgqk/dot_general | solution.py:58
  91.5 3.7 %fusion.65 = f32[1,4,512,64]{2,3,1,0:T(8,128)S(1)} fusion(f32[512,512,4]{1,0,2:T(8,128)} %get-tuple-element.358, f32[4,512]{1,0:T(4,128)S(1)} %bitcast.99, pred[512,512]{0,1:T(8,128)(4,1)S(1)} %broadcast_compare_fusion.3, f32[1,4,512,64]{2,3,1,0:T(8,128)S(1)} %get-tuple-element.376, f32[4,512]{1,0:T(4,128)S(1)} %get-tuple-element.359, ...), kind=kOutput, calls=%fused_computation.9.clone.1 | convolution fusion | flops 139853824 | bytes 5586953 | tf_op jit(solution)/shard_map/while/body/eval_jaxpr/hgqk,khd->hgqd/dot_general | solution.py:67
  95.3 1.0 fusion.64
  96.4 0.3 convert_element_type.40
  96.7 0.3 copy.15
  97.0 9.4 %all_to_all.16 = bf16[8,64,256]{2,1,0:T(8,128)(2,1)S(1)} all-to-all(bf16[8,64,256]{2,1,0:T(8,128)(2,1)S(1)} %copy.15), channel_id=1, replica_groups=mesh['grp'=4,'sp'=8] {'sp'}, dimensions={0} | all-to-all | bytes 524288 | tf_op jit(solution)/shard_map/all_to_all | solution.py:127
  106.5 0.7 copy.18
  (47 shorter events, 0.8 us)
Async XLA Ops:
  6.5 37.1 %all-gather.2.cloned.1.call-start = ((), (), s32[]{:S(2)}) async-start(), calls=%async_computation.1 | async-start | bytes 3391488 | tf_op jit(solution)/shard_map/all_gather | solution.py:95
  43.6 20.8 %copy-start.1 = (s32[16]{0:T(128)S(1)}, s32[16]{0:T(128)}, u32[]{:S(2)}) copy-start(s32[16]{0:T(128)} %param.10) | copy-start | bytes 196
  67.5 3.7 %copy-start = (f32[512,512,4]{1,0,2:T(8,128)S(1)}, f32[512,512,4]{1,0,2:T(8,128)}, u32[]{:S(2)}) copy-start(f32[512,512,4]{1,0,2:T(8,128)} %get-tuple-element.358) | copy-start | bytes 12582916 | tf_op jit(solution)/shard_map/while
  75.5 3.7 %copy-start = (f32[512,512,4]{1,0,2:T(8,128)S(1)}, f32[512,512,4]{1,0,2:T(8,128)}, u32[]{:S(2)}) copy-start(f32[512,512,4]{1,0,2:T(8,128)} %get-tuple-element.358) | copy-start | bytes 12582916 | tf_op jit(solution)/shard_map/while
  83.5 3.7 %copy-start = (f32[512,512,4]{1,0,2:T(8,128)S(1)}, f32[512,512,4]{1,0,2:T(8,128)}, u32[]{:S(2)}) copy-start(f32[512,512,4]{1,0,2:T(8,128)} %get-tuple-element.358) | copy-start | bytes 12582916 | tf_op jit(solution)/shard_map/while
  91.5 3.7 %copy-start = (f32[512,512,4]{1,0,2:T(8,128)S(1)}, f32[512,512,4]{1,0,2:T(8,128)}, u32[]{:S(2)}) copy-start(f32[512,512,4]{1,0,2:T(8,128)} %get-tuple-element.358) | copy-start | bytes 12582916 | tf_op jit(solution)/shard_map/while
Sparse Core Ops, SparseCore 0:
  9.2 34.3 all-gather.1
where the time goes:
time: 114 us
  waiting for transfers between devices  33.3 us (29%)
  matrix products  30.1 us (26%)
  blocking collectives  25.5 us (22%)
  between operations  13.6 us (12%)
  other arithmetic  7.27 us (6%)
  local copies, waits for them, and re-layouts  4.05 us (4%)
    all_gather x1, waiting for transfers between devices, per_device(): lax.all_gather(tokens, 'sp', axis=0, tiled=True)  32.6 us
    all_gather x1, blocking collectives, per_device(): piece = lax.all_gather(key_value_pair, 'grp', axis=0, tiled=True)  16 us
    dot_general x4, matrix products, attend(): jnp.einsum('hgqk,khd->hgqd', weights.astype(jnp.bfloat16), value_part, pr...  14.8 us
    dot_general x4, matrix products, attend(): jnp.einsum('qhgd,khd->hgqk', queries, key_part, preferred_element_type=jn...  11.2 us
    all_to_all x1, blocking collectives, per_device(): lax.all_to_all(attended, 'sp', split_axis=0, concat_axis=1, tiled=True)  9.44 us
    reduce_sum x4, other arithmetic, attend(): totals = totals * factor + jnp.sum(weights, axis=-1)  4.17 us
    dot_general x1, matrix products, per_device(): jnp.dot(lax.all_gather(tokens, 'sp', axis=0, tiled=True), joined, preferr...  4.11 us
  transfers between devices with their start and end apart: 1, of which 1 were waited for; matrix products, arithmetic and copies ran while one was open for 3% of the time, Pallas kernels for 0%

commit v1 on v0

--- a/solution.py
+++ b/solution.py
@@ -109,7 +109,21 @@
         jnp.ones((head_count, query_sharing, group_rows), jnp.float32),
         jnp.zeros((head_count, query_sharing, group_rows, HEAD_SIZE), jnp.float32),
     )
-    piece = lax.all_gather(key_value_pair, "grp", axis=0, tiled=True)
+
+    def plan_the_heads(row_dim, vals):
+        degree = jax.lax.axis_size("grp")
+        everything = list(map(lambda ix: (ix - 1, ix), range(1, degree))) + [(degree - 1, 0)]
+        newest = vals
+        series = [newest]
+        for _ in range(degree - 1):
+            newest = jax.lax.ppermute(newest, "grp", everything)
+            series += [newest]
+        item_now = jnp.concatenate([*reversed(series)], row_dim)
+        return jnp.roll(
+            item_now, (jax.lax.axis_index("grp") + 1) * newest.shape[row_dim], axis=row_dim
+        )
+
+    piece = plan_the_heads(0, key_value_pair)
     step_rows = min(piece.shape[0], group_rows)
     turns = piece.shape[0] // step_rows
 

time: 114 us -> 119 us (1.044)
  waiting for transfers between devices: 33.3 us -> 53.4 us
  blocking collectives: 25.5 us -> 9.44 us
  starting transfers between devices: 0.01 us -> 1.54 us
    ppermute x0 -> x3, waiting for transfers between devices: none -> 18.9 us  [plan_the_heads(): newest = jax.lax.ppermute(newest, 'grp', everything)]
    all_gather x1 -> x0, blocking collectives: 16 us -> none  [per_device(): piece = lax.all_gather(key_value_pair, 'grp', axis=0, tiled=True)]
    ppermute x0 -> x3, starting transfers between devices: none -> 1.54 us  [plan_the_heads(): newest = jax.lax.ppermute(newest, 'grp', everything)]
  transfers between devices with their start and end apart: 1 -> 4, of which waited for: 1 -> 4; matrix products, arithmetic and copies ran while one was open for 3% -> 3% of each run, Pallas kernels for 0% -> 0%
where the time goes in v1:
time: 119 us
  waiting for transfers between devices  53.4 us (45%)
  matrix products  30.1 us (25%)
  between operations  13.6 us (11%)
  blocking collectives  9.44 us (8%)
  other arithmetic  7.29 us (6%)
  local copies, waits for them, and re-layouts  3.49 us (3%)
  starting transfers between devices  1.54 us (1%)
    all_gather x1, waiting for transfers between devices, per_device(): lax.all_gather(tokens, 'sp', axis=0, tiled=True)  33.7 us
    ppermute x3, waiting for transfers between devices, plan_the_heads(): newest = jax.lax.ppermute(newest, 'grp', everything)  18.9 us
    dot_general x4, matrix products, attend(): jnp.einsum('hgqk,khd->hgqd', weights.astype(jnp.bfloat16), value_part, pr...  14.8 us
    dot_general x4, matrix products, attend(): jnp.einsum('qhgd,khd->hgqk', queries, key_part, preferred_element_type=jn...  11.1 us
    all_to_all x1, blocking collectives, per_device(): lax.all_to_all(attended, 'sp', split_axis=0, concat_axis=1, tiled=True)  9.44 us
    reduce_sum x4, other arithmetic, attend(): totals = totals * factor + jnp.sum(weights, axis=-1)  4.17 us
    dot_general x1, matrix products, per_device(): jnp.dot(lax.all_gather(tokens, 'sp', axis=0, tiled=True), joined, preferr...  4.1 us
  transfers between devices with their start and end apart: 4, of which 4 were waited for; matrix products, arithmetic and copies ran while one was open for 3% of the time, Pallas kernels for 0%

profile of v1, /device:TPU:0, one launch (start us, length us, event | category | flops | bytes accessed | tf_op | source)
XLA Modules:
  0.0 119.1 jit_solution(15063231160592752952)
XLA Ops:
  6.5 0.7 all-gather.2.cloned.1.call-update
  7.3 0.7 select_reduce_fusion.1
  8.1 1.8 %constant_dynamic-slice_fusion.2 = (bf16[2880,64]{1,0:T(8,128)(2,1)S(1)}, bf16[2880,64]{1,0:T(8,128)(2,1)S(1)}) fusion(bf16[2880,1024]{1,0:T(8,128)(2,1)} %param.9, s32[]{:T(128)S(6)} %select_n.175, s32[]{:T(128)S(6)} %select_n.176), kind=kLoop, calls=%fused_computation.100 | loop fusion | bytes 1474568 | tf_op jit(solution)/shard_map/dynamic_slice | solution.py:89
  9.9 33.7 %all-gather.2.cloned.1.call-done = bf16[512,2880]{1,0:T(8,128)(2,1)} async-done(((bf16[64,2880]{1,0:T(8,128)(2,1)}), bf16[512,2880]{1,0:T(8,128)(2,1)}) %all-gather.2.cloned.1.call-update) | async-done | bytes 2949136 | tf_op jit(solution)/shard_map/all_gather | solution.py:95
  43.6 4.1 %fusion.32 = f32[512,384]{0,1:T(8,128)S(1)} fusion(bf16[512,2880]{1,0:T(8,128)(2,1)} %all-gather.2.cloned.1.call-done, bf16[2880,64]{1,0:T(8,128)(2,1)S(1)} %get-tuple-element.296, bf16[2880,64]{1,0:T(8,128)(2,1)S(1)} %get-tuple-element.295, bf16[2880,256]{1,0:T(8,128)(2,1)} %param.8), kind=kOutput, calls=%fused_computation.53 | convolution fusion | flops 1139097600 | bytes 5947392 | tf_op jit(solution)/shard_map/dot_general | solution.py:94
  47.8 0.3 fusion.43
  48.1 1.5 %collective-permute-start = (bf16[512,128]{0,1:T(8,128)(2,1)S(1)}, bf16[512,128]{0,1:T(8,128)(2,1)S(1)}, u32[]{:S(2)}, u32[]{:S(2)}) collective-permute-start(bf16[512,128]{0,1:T(8,128)(2,1)S(1)} %pad_maximum_fusion.1), channel_id=1, source_target_pairs={{0,8},{8,16},{16,24},{24,0},{1,9},{9,17},{17,25},{25,1},{2,10},{10... | collective-permute-start | bytes 393224 | tf_op jit(solution)/shard_map/ppermute | solution.py:119
  49.7 5.9 %collective-permute-done = bf16[512,128]{0,1:T(8,128)(2,1)S(1)} collective-permute-done((bf16[512,128]{0,1:T(8,128)(2,1)S(1)}, bf16[512,128]{0,1:T(8,128)(2,1)S(1)}, u32[]{:S(2)}, u32[]{:S(2)}) %collective-permute-start) | collective-permute-done | bytes 131104 | tf_op jit(solution)/shard_map/ppermute | solution.py:119
  55.6 0.3 multiply_cosine_fusion
  56.0 6.4 %collective-permute-done.1 = bf16[512,128]{0,1:T(8,128)(2,1)S(1)} collective-permute-done((bf16[512,128]{0,1:T(8,128)(2,1)S(1)}, bf16[512,128]{0,1:T(8,128)(2,1)S(1)}, u32[]{:S(2)}, u32[]{:S(2)}) %collective-permute-start.1) | collective-permute-done | bytes 131104 | tf_op jit(solution)/shard_map/ppermute | solution.py:119
  62.5 6.7 %collective-permute-done.2 = bf16[512,128]{0,1:T(8,128)(2,1)S(1)} collective-permute-done((bf16[512,128]{0,1:T(8,128)(2,1)S(1)}, bf16[512,128]{0,1:T(8,128)(2,1)S(1)}, u32[]{:S(2)}, u32[]{:S(2)}) %collective-permute-start.2) | collective-permute-done | bytes 131104 | tf_op jit(solution)/shard_map/ppermute | solution.py:119
  69.4 32.0 %while.21 = (s32[]{:T(128)}, f32[1,4,512]{2,1,0:T(4,128)S(1)}, f32[1,4,512]{2,1,0:T(4,128)S(1)}, f32[1,4,512,64]{2,3,1,0:T(8,128)S(1)}, s32[16]{0:T(128)S(1)}, /...) while((s32[]{:T(128)}, f32[1,4,512]{2,1,0:T(4,128)S(1)}, ...), condition=%wide.region_5.6_spmd.clone, body=%wide.region_1.5_spmd.clone.sunk | while | flops 282791424 | bytes 31996208 | solution.py:138
  69.6 0.2 broadcast_compare_fusion.3
  69.8 2.8 %fusion.62 = (f32[4,512]{1,0:T(4,128)S(1)}, f32[512,512,4]{1,0,2:T(8,128)}) fusion(pred[512,512]{0,1:T(8,128)(4,1)S(1)} %broadcast_compare_fusion.3, bf16[512,1,4,64]{0,3,2,1:T(8,128)(2,1)S(1)} %get-tuple-element.393, bf16[2048,128]{0,1:T(8,128)(2,1)S(1)} %get-tuple-element.392, s32[]{:T(128)S(6)} %select_n.270), kind=kOutput, calls=%fused_computation.2.clone.1 | convolution fusion | flops 137361408 | bytes 4792324 | tf_op jit(solution)/shard_map/while/body/eval_jaxpr/qhgd,khd->hgqk/dot_general | solution.py:58
  72.6 3.7 %fusion.65 = f32[1,4,512,64]{2,3,1,0:T(8,128)S(1)} fusion(f32[512,512,4]{1,0,2:T(8,128)} %get-tuple-element.358, f32[4,512]{1,0:T(4,128)S(1)} %bitcast.99, pred[512,512]{0,1:T(8,128)(4,1)S(1)} %broadcast_compare_fusion.3, f32[1,4,512,64]{2,3,1,0:T(8,128)S(1)} %get-tuple-element.376, f32[4,512]{1,0:T(4,128)S(1)} %get-tuple-element.359, ...), kind=kOutput, calls=%fused_computation.9.clone.1 | convolution fusion | flops 139853824 | bytes 5586953 | tf_op jit(solution)/shard_map/while/body/eval_jaxpr/hgqk,khd->hgqd/dot_general | solution.py:67
  76.3 1.0 fusion.64
  77.5 0.2 broadcast_compare_fusion.3
  77.8 2.8 %fusion.62 = (f32[4,512]{1,0:T(4,128)S(1)}, f32[512,512,4]{1,0,2:T(8,128)}) fusion(pred[512,512]{0,1:T(8,128)(4,1)S(1)} %broadcast_compare_fusion.3, bf16[512,1,4,64]{0,3,2,1:T(8,128)(2,1)S(1)} %get-tuple-element.393, bf16[2048,128]{0,1:T(8,128)(2,1)S(1)} %get-tuple-element.392, s32[]{:T(128)S(6)} %select_n.270), kind=kOutput, calls=%fused_computation.2.clone.1 | convolution fusion | flops 137361408 | bytes 4792324 | tf_op jit(solution)/shard_map/while/body/eval_jaxpr/qhgd,khd->hgqk/dot_general | solution.py:58
  80.6 3.7 %fusion.65 = f32[1,4,512,64]{2,3,1,0:T(8,128)S(1)} fusion(f32[512,512,4]{1,0,2:T(8,128)} %get-tuple-element.358, f32[4,512]{1,0:T(4,128)S(1)} %bitcast.99, pred[512,512]{0,1:T(8,128)(4,1)S(1)} %broadcast_compare_fusion.3, f32[1,4,512,64]{2,3,1,0:T(8,128)S(1)} %get-tuple-element.376, f32[4,512]{1,0:T(4,128)S(1)} %get-tuple-element.359, ...), kind=kOutput, calls=%fused_computation.9.clone.1 | convolution fusion | flops 139853824 | bytes 5586953 | tf_op jit(solution)/shard_map/while/body/eval_jaxpr/hgqk,khd->hgqd/dot_general | solution.py:67
  84.3 1.0 fusion.64
  85.5 0.2 broadcast_compare_fusion.3
  85.8 2.8 %fusion.62 = (f32[4,512]{1,0:T(4,128)S(1)}, f32[512,512,4]{1,0,2:T(8,128)}) fusion(pred[512,512]{0,1:T(8,128)(4,1)S(1)} %broadcast_compare_fusion.3, bf16[512,1,4,64]{0,3,2,1:T(8,128)(2,1)S(1)} %get-tuple-element.393, bf16[2048,128]{0,1:T(8,128)(2,1)S(1)} %get-tuple-element.392, s32[]{:T(128)S(6)} %select_n.270), kind=kOutput, calls=%fused_computation.2.clone.1 | convolution fusion | flops 137361408 | bytes 4792324 | tf_op jit(solution)/shard_map/while/body/eval_jaxpr/qhgd,khd->hgqk/dot_general | solution.py:58
  88.6 3.7 %fusion.65 = f32[1,4,512,64]{2,3,1,0:T(8,128)S(1)} fusion(f32[512,512,4]{1,0,2:T(8,128)} %get-tuple-element.358, f32[4,512]{1,0:T(4,128)S(1)} %bitcast.99, pred[512,512]{0,1:T(8,128)(4,1)S(1)} %broadcast_compare_fusion.3, f32[1,4,512,64]{2,3,1,0:T(8,128)S(1)} %get-tuple-element.376, f32[4,512]{1,0:T(4,128)S(1)} %get-tuple-element.359, ...), kind=kOutput, calls=%fused_computation.9.clone.1 | convolution fusion | flops 139853824 | bytes 5586953 | tf_op jit(solution)/shard_map/while/body/eval_jaxpr/hgqk,khd->hgqd/dot_general | solution.py:67
  92.3 1.0 fusion.64
  93.5 0.2 broadcast_compare_fusion.3
  93.8 2.8 %fusion.62 = (f32[4,512]{1,0:T(4,128)S(1)}, f32[512,512,4]{1,0,2:T(8,128)}) fusion(pred[512,512]{0,1:T(8,128)(4,1)S(1)} %broadcast_compare_fusion.3, bf16[512,1,4,64]{0,3,2,1:T(8,128)(2,1)S(1)} %get-tuple-element.393, bf16[2048,128]{0,1:T(8,128)(2,1)S(1)} %get-tuple-element.392, s32[]{:T(128)S(6)} %select_n.270), kind=kOutput, calls=%fused_computation.2.clone.1 | convolution fusion | flops 137361408 | bytes 4792324 | tf_op jit(solution)/shard_map/while/body/eval_jaxpr/qhgd,khd->hgqk/dot_general | solution.py:58
  96.6 3.7 %fusion.65 = f32[1,4,512,64]{2,3,1,0:T(8,128)S(1)} fusion(f32[512,512,4]{1,0,2:T(8,128)} %get-tuple-element.358, f32[4,512]{1,0:T(4,128)S(1)} %bitcast.99, pred[512,512]{0,1:T(8,128)(4,1)S(1)} %broadcast_compare_fusion.3, f32[1,4,512,64]{2,3,1,0:T(8,128)S(1)} %get-tuple-element.376, f32[4,512]{1,0:T(4,128)S(1)} %get-tuple-element.359, ...), kind=kOutput, calls=%fused_computation.9.clone.1 | convolution fusion | flops 139853824 | bytes 5586953 | tf_op jit(solution)/shard_map/while/body/eval_jaxpr/hgqk,khd->hgqd/dot_general | solution.py:67
  100.3 1.0 fusion.64
  101.4 0.3 convert_element_type.40
  101.7 0.3 copy.15
  102.1 9.4 %all_to_all.16 = bf16[8,64,256]{2,1,0:T(8,128)(2,1)S(1)} all-to-all(bf16[8,64,256]{2,1,0:T(8,128)(2,1)S(1)} %copy.15), channel_id=1, replica_groups=mesh['grp'=4,'sp'=8] {'sp'}, dimensions={0} | all-to-all | bytes 524288 | tf_op jit(solution)/shard_map/all_to_all | solution.py:141
  111.5 0.7 copy.18
  (63 shorter events, 1.2 us)
Async XLA Ops:
  6.5 37.1 %all-gather.2.cloned.1.call-start = ((), (), s32[]{:S(2)}) async-start(), calls=%async_computation.1 | async-start | bytes 3391488 | tf_op jit(solution)/shard_map/all_gather | solution.py:95
  43.6 6.1 %copy-start.2 = (f32[32]{0:T(128)S(1)}, f32[32]{0:T(128)}, u32[]{:S(2)}) copy-start(f32[32]{0:T(128)} %param.11) | copy-start | bytes 388
  47.7 21.7 %copy-start.1 = (s32[16]{0:T(128)S(1)}, s32[16]{0:T(128)}, u32[]{:S(2)}) copy-start(s32[16]{0:T(128)} %param.10) | copy-start | bytes 196
  48.1 7.5 %collective-permute-start = (bf16[512,128]{0,1:T(8,128)(2,1)S(1)}, bf16[512,128]{0,1:T(8,128)(2,1)S(1)}, u32[]{:S(2)}, u32[]{:S(2)}) collective-permute-start(bf16[512,128]{0,1:T(8,128)(2,1)S(1)} %pad_maximum_fusion.1), channel_id=1, source_target_pairs={{0,8},{8,16},{16,24},{24,0},{1,9},{9,17},{17,25},{25,1},{2,10},{10... | collective-permute-start | bytes 393224 | tf_op jit(solution)/shard_map/ppermute | solution.py:119
  55.6 6.8 %collective-permute-start.1 = (bf16[512,128]{0,1:T(8,128)(2,1)S(1)}, bf16[512,128]{0,1:T(8,128)(2,1)S(1)}, u32[]{:S(2)}, u32[]{:S(2)}) collective-permute-start(bf16[512,128]{0,1:T(8,128)(2,1)S(1)} %collective-permute-done), channel_id=1, source_target_pairs={{0,8},{8,16},{16,24},{24,0},{1,9},{9,17},{17,25},{25,1},{2,10},{10... | collective-permute-start | bytes 393224 | tf_op jit(solution)/shard_map/ppermute | solution.py:119
  62.4 6.8 %collective-permute-start.2 = (bf16[512,128]{0,1:T(8,128)(2,1)S(1)}, bf16[512,128]{0,1:T(8,128)(2,1)S(1)}, u32[]{:S(2)}, u32[]{:S(2)}) collective-permute-start(bf16[512,128]{0,1:T(8,128)(2,1)S(1)} %collective-permute-done.1), channel_id=1, source_target_pairs={{0,8},{8,16},{16,24},{24,0},{1,9},{9,17},{17,25},{25,1},{2,10},{10... | collective-permute-start | bytes 393224 | tf_op jit(solution)/shard_map/ppermute | solution.py:119
  72.6 3.7 %copy-start = (f32[512,512,4]{1,0,2:T(8,128)S(1)}, f32[512,512,4]{1,0,2:T(8,128)}, u32[]{:S(2)}) copy-start(f32[512,512,4]{1,0,2:T(8,128)} %get-tuple-element.358) | copy-start | bytes 12582916 | tf_op jit(solution)/shard_map/while
  80.6 3.7 %copy-start = (f32[512,512,4]{1,0,2:T(8,128)S(1)}, f32[512,512,4]{1,0,2:T(8,128)}, u32[]{:S(2)}) copy-start(f32[512,512,4]{1,0,2:T(8,128)} %get-tuple-element.358) | copy-start | bytes 12582916 | tf_op jit(solution)/shard_map/while
  88.6 3.7 %copy-start = (f32[512,512,4]{1,0,2:T(8,128)S(1)}, f32[512,512,4]{1,0,2:T(8,128)}, u32[]{:S(2)}) copy-start(f32[512,512,4]{1,0,2:T(8,128)} %get-tuple-element.358) | copy-start | bytes 12582916 | tf_op jit(solution)/shard_map/while
  96.6 3.7 %copy-start = (f32[512,512,4]{1,0,2:T(8,128)S(1)}, f32[512,512,4]{1,0,2:T(8,128)}, u32[]{:S(2)}) copy-start(f32[512,512,4]{1,0,2:T(8,128)} %get-tuple-element.358) | copy-start | bytes 12582916 | tf_op jit(solution)/shard_map/while
Sparse Core Ops, SparseCore 0:
  9.2 34.3 all-gather.1
